TPU v7x, 128 devices: a whole 4x4x4 slice. The times are simulated.
128 devices in a mesh: row: 8 (over y, z_lo), col: 16 (over z_hi, x, core).
Axes of the slice: x: 4, y: 4, z: 4 (z_hi: 2, z_lo: 2; z = z_hi * 2 + z_lo), core: 2. Of those that a mesh axis runs over, the one named last changes fastest.
Arguments:
- spectra: bfloat16 [16, 2048, 2048], P('row', None, 'col'), may hold values from -6 to 6
- coupling: float32 [16], replicated, may hold values from 0.2 to 1
Outputs:
- returned_spectra: bfloat16 [16, 2048, 2048], P('row', None, 'col')
All inputs are finite; a program needn't handle non-finite values.
Results may differ from a plain program's by a relative error of at most 0.0079.
Values may be sent and summed in bfloat16 or wider, within the bound.
A program may use at most 128 MiB of HBM per device.

v0:
```python
import math

import jax
import jax.numpy as jnp
from jax import lax
from jax.sharding import Mesh
from jax.sharding import PartitionSpec as P

NX = 3072
NY = 3072
M = 1024
COL = ("col_0", "col_1", "col_2")


def in_blocks(array, dim, peers):
    dims = array.shape
    tiles = array.reshape(*dims[:dim], peers, dims[dim] // peers, *dims[dim + 1 :])
    return jnp.moveaxis(tiles, dim, 0)


def joined_along(tiles, dim):
    dims = list(tiles.shape[1:])
    dims[dim] *= tiles.shape[0]
    return jnp.moveaxis(tiles, 0, dim).reshape(dims)


def moved_by_axis(tiles, axes, turns):
    dims = [lax.axis_size(a) for a in axes]
    tiles = tiles.reshape(*dims, *tiles.shape[1:])
    for k in turns:
        tiles = lax.all_to_all(tiles, axes[k], split_axis=k, concat_axis=k, tiled=True)
    return tiles.reshape(-1, *tiles.shape[len(axes) :])


def core_and_chips(array, groups, turns, split_dim, concat_dim):
    peers = lax.axis_size(groups[0]) * lax.axis_size(groups[1])
    tiles = in_blocks(array, split_dim, peers)
    return joined_along(moved_by_axis(tiles, groups, turns), concat_dim)


def fourier_rows(mode_count, length, factor):
    wavenumber = jnp.arange(1, mode_count + 1, dtype=jnp.int32)
    position = jnp.arange(length, dtype=jnp.int32)
    residue = wavenumber[:, None] * position[None, :] % length
    angles = residue.astype(jnp.float32) * (2.0 * math.pi / length)
    table = jnp.concatenate([jnp.cos(angles), jnp.sin(angles)], 0) * factor
    return table.astype(jnp.bfloat16)


def ellipse(row_index, column_index, mode_count):
    row_waves = row_index % mode_count + 1
    col_waves = column_index % mode_count + 1
    inside = (
        row_waves[:, None] * row_waves[:, None] + col_waves[None, :] * col_waves[None, :]
        <= mode_count * mode_count
    )
    return inside.astype(jnp.float32)


def on_device(spectra, coupling):
    local_count = spectra.shape[0]
    width_here = spectra.shape[2]
    inverse_y = fourier_rows(M, NY, 1.0 / math.sqrt(M)).T
    inverse_x = fourier_rows(M, NX, 1.0 / math.sqrt(M))
    forward_x = fourier_rows(M, NX, 2.0 * math.sqrt(M) / NX).T
    forward_y = fourier_rows(M, NY, 2.0 * math.sqrt(M) / NY)
    half_done = jnp.einsum(
        "yk,fkc->fyc", inverse_y, spectra, preferred_element_type=jnp.float32
    ).astype(jnp.bfloat16)
    gathered = core_and_chips(half_done, (("col_0", "col_1"), "col_2"), (1, 0), 1, 2)
    first_field = lax.axis_index("row") * local_count
    strength = lax.dynamic_slice_in_dim(coupling, first_field, gathered.shape[0])
    gridded = jnp.einsum("fyk,kx->fyx", gathered, inverse_x, preferred_element_type=jnp.float32)
    tendency = (gridded + strength[:, None, None] * gridded * gridded).astype(jnp.bfloat16)
    projected = jnp.einsum(
        "fyx,xk->fyk", tendency, forward_x, preferred_element_type=jnp.float32
    ).astype(jnp.bfloat16)
    returned = lax.all_to_all(projected, COL, split_axis=2, concat_axis=1, tiled=True)
    result = jnp.einsum("ky,fyc->fkc", forward_y, returned, preferred_element_type=jnp.float32)
    columns = lax.axis_index(COL) * width_here + jnp.arange(width_here, dtype=jnp.int32)
    inside = ellipse(jnp.arange(2 * M, dtype=jnp.int32), columns, M)
    return (result * inside[None, :, :]).astype(jnp.bfloat16)


def solution(mesh):
    torus = Mesh(
        mesh.devices.reshape(mesh.shape["row"], 2, 4, 2), ("row", "col_0", "col_1", "col_2")
    )
    return jax.shard_map(
        on_device,
        mesh=torus,
        in_specs=(P("row", None, COL), P()),
        out_specs=P("row", None, COL),
        check_vma=False,
    )
```

profile of v0, /device:TPU:1, one launch (start us, length us, event | category | flops | bytes accessed | tf_op | source)
XLA Modules:
  0.0 182.3 jit_solution(15126641113345682228)
XLA Ops:
  0.0 0.0 copy-start
  0.0 52.6 %fusion.7 = (f32[1024,3072]{0,1:T(8,128)}, f32[1024,3072]{0,1:T(8,128)}) fusion(s32[1024]{0:T(1024)S(1)} %iota_add_fusion), kind=kLoop, calls=%fused_computation.12 | loop fusion | flops 28311552 | bytes 25169920 | tf_op jit(solution)/shard_map/cos | solution.py:46
  52.6 0.0 copy-done
  52.6 10.0 %convolution_convert_fusion = bf16[3072,2,128]{2,0,1:T(8,128)(2,1)S(1)} fusion(bf16[2,2048,128]{2,1,0:T(8,128)(2,1)S(1)} %copy-done, f32[1024,3072]{0,1:T(8,128)} %get-tuple-element.6, f32[1024,3072]{0,1:T(8,128)} %get-tuple-element.5), kind=kOutput, calls=%fused_computation.16 | convolution fusion | flops 3240886272 | bytes 27787264 | tf_op jit(solution)/shard_map/yk,fkc->fyc/dot_general | solution.py:67
  62.6 0.0 copy-start.1
  62.6 0.1 copy.24
  62.8 6.0 %all_to_all.28 = bf16[8,2,2,192,128]{4,3,0,2,1:T(8,128)(2,1)S(1)} all-to-all(bf16[8,2,2,192,128]{4,3,0,2,1:T(8,128)(2,1)S(1)} %copy.24), channel_id=1, replica_groups=mesh['row'=8,'col_0'=2,'col_1'=4,'col_2'=2] {'col_2'}, dimensions={1} | all-to-all | bytes 3145728 | tf_op jit(solution)/shard_map/all_to_all | solution.py:31
  68.8 1.3 copy.25
  70.1 7.4 %all-to-all-start.1 = ((bf16[8,2,2,192,128]{4,3,1,2,0:T(8,128)(2,1)}), bf16[8,2,2,192,128]{4,3,1,2,0:T(8,128)(2,1)S(1)}, u32[]{:S(2)}, u32[]{:S(2)}) async-start(bf16[8,2,2,192,128]{4,3,1,2,0:T(8,128)(2,1)} %copy.25), calls=%async_computation.1 | async-start | bytes 3145728 | tf_op jit(solution)/shard_map/all_to_all | solution.py:31
  77.6 0.0 copy-done.1
  77.6 0.1 dynamic_slice.3
  77.7 22.9 %all-to-all-done.1 = bf16[8,2,2,192,128]{4,3,1,2,0:T(8,128)(2,1)S(1)} async-done(((bf16[8,2,2,192,128]{4,3,1,2,0:T(8,128)(2,1)}), bf16[8,2,2,192,128]{4,3,1,2,0:T(8,128)(2,1)S(1)}, u32[]{:S(2)}, u32[]{:S(2)}) %all-to-all-start.1) | async-done | bytes 1572896 | tf_op jit(solution)/shard_map/all_to_all | solution.py:31
  100.6 1.3 copy.26
  101.8 12.3 %fusion.9 = bf16[2,192,3072]{2,1,0:T(8,128)(2,1)} fusion(f32[2]{0:T(128)S(1)} %dynamic_slice.3, f32[1024,3072]{0,1:T(8,128)} %get-tuple-element.6, f32[1024,3072]{0,1:T(8,128)} %get-tuple-element.5, bf16[16,2,24,8,128]{4,3,2,1,0:T(8,128)(2,1)} %bitcast.40), kind=kOutput, calls=%fused_computation.15 | convolution fusion | flops 4855431168 | bytes 29097992 | tf_op jit(solution)/shard_map/fyk,kx->fyx/dot_general | solution.py:73
  114.1 13.9 %convolution_convert_fusion.1 = bf16[2,192,2048]{2,1,0:T(8,128)(2,1)S(1)} fusion(bf16[2,192,3072]{2,1,0:T(8,128)(2,1)} %fusion.9, f32[1024,3072]{0,1:T(8,128)} %get-tuple-element.6, f32[1024,3072]{0,1:T(8,128)} %get-tuple-element.5), kind=kOutput, calls=%fused_computation.17 | convolution fusion | flops 4851499008 | bytes 29097984 | tf_op jit(solution)/shard_map/fyx,xk->fyk/dot_general | solution.py:75
  128.1 3.8 %copy.30 = bf16[2,192,2048]{1,0,2:T(2,128)(2,1)} copy(bf16[2,192,2048]{2,1,0:T(8,128)(2,1)S(1)} %convolution_convert_fusion.1) | data formatting | bytes 3145728 | tf_op jit(solution)/shard_map/convert_element_type | solution.py:77
  131.9 4.6 %all-to-all-start.2 = ((bf16[2,192,2048]{1,0,2:T(2,128)(2,1)}), bf16[2,192,2048]{1,0,2:T(2,128)(2,1)S(1)}, u32[]{:S(2)}, u32[]{:S(2)}) async-start(bf16[2,192,2048]{1,0,2:T(2,128)(2,1)} %copy.30), calls=%async_computation.2 | async-start | bytes 4194304 | tf_op jit(solution)/shard_map/all_to_all | solution.py:78
  136.5 1.1 fusion.18
  137.7 27.3 %all-to-all-done.2 = bf16[2,192,2048]{1,0,2:T(2,128)(2,1)S(1)} async-done(((bf16[2,192,2048]{1,0,2:T(2,128)(2,1)}), bf16[2,192,2048]{1,0,2:T(2,128)(2,1)S(1)}, u32[]{:S(2)}, u32[]{:S(2)}) %all-to-all-start.2) | async-done | bytes 1572896 | tf_op jit(solution)/shard_map/all_to_all | solution.py:78
  165.0 3.7 %copy.44 = bf16[2,192,16,128]{3,1,2,0:T(8,128)(2,1)} copy(bf16[2,192,16,128]{1,0,3,2:T(2,128)(2,1)S(1)} %bitcast.38) | data formatting | bytes 3145728 | tf_op jit(solution)/shard_map/all_to_all | solution.py:78
  168.7 12.3 %fusion.11 = bf16[2,2048,128]{1,2,0:T(8,128)(2,1)S(1)} fusion(bf16[2,3072,128]{2,1,0:T(8,128)(2,1)} %bitcast.39, f32[1024,3072]{0,1:T(8,128)} %get-tuple-element.6, f32[1024,3072]{0,1:T(8,128)} %get-tuple-element.5, f32[2048,128]{0,1:T(8,128)} %fusion.18), kind=kOutput, calls=%fused_computation.20 | convolution fusion | flops 3241148416 | bytes 28835840 | tf_op jit(solution)/shard_map/ky,fyc->fkc/dot_general | solution.py:79
  181.0 1.3 copy.35
  (3 shorter events, 0.0 us)
Async XLA Ops:
  0.0 52.6 %copy-start = (bf16[2,2048,128]{2,1,0:T(8,128)(2,1)S(1)}, bf16[2,2048,128]{2,1,0:T(8,128)(2,1)}, u32[]{:S(2)}) copy-start(bf16[2,2048,128]{2,1,0:T(8,128)(2,1)} %param.2) | copy-start | bytes 3145732
  62.6 14.9 %copy-start.1 = (f32[16]{0:T(128)S(1)}, f32[16]{0:T(128)}, u32[]{:S(2)}) copy-start(f32[16]{0:T(128)} %param.3) | copy-start | bytes 196
  70.1 30.4 %all-to-all-start.1 = ((bf16[8,2,2,192,128]{4,3,1,2,0:T(8,128)(2,1)}), bf16[8,2,2,192,128]{4,3,1,2,0:T(8,128)(2,1)S(1)}, u32[]{:S(2)}, u32[]{:S(2)}) async-start(bf16[8,2,2,192,128]{4,3,1,2,0:T(8,128)(2,1)} %copy.25), calls=%async_computation.1 | async-start | bytes 3145728 | tf_op jit(solution)/shard_map/all_to_all | solution.py:31
  131.9 33.1 %all-to-all-start.2 = ((bf16[2,192,2048]{1,0,2:T(2,128)(2,1)}), bf16[2,192,2048]{1,0,2:T(2,128)(2,1)S(1)}, u32[]{:S(2)}, u32[]{:S(2)}) async-start(bf16[2,192,2048]{1,0,2:T(2,128)(2,1)} %copy.30), calls=%async_computation.2 | async-start | bytes 4194304 | tf_op jit(solution)/shard_map/all_to_all | solution.py:78
where the time goes:
time: 183 us; the launch traced here: 182 us
  other arithmetic  53.8 us (29%)
  waiting for transfers between devices  50.2 us (27%)
  matrix products  48.6 us (27%)
  starting transfers between devices  12.1 us (7%)
  local copies, waits for them, and re-layouts  11.6 us (6%)
  blocking collectives  6 us (3%)
    cos x1, other arithmetic, fourier_rows(): table = jnp.concatenate([jnp.cos(angles), jnp.sin(angles)], 0) * factor  52.6 us
    all_to_all x1, waiting for transfers between devices, on_device(): lax.all_to_all(projected, COL, split_axis=2, concat_axis=1, tiled=True)  27.3 us
    all_to_all x1, waiting for transfers between devices, moved_by_axis(): lax.all_to_all(tiles, axes[k], split_axis=k, concat_axis=k, tiled=True)  22.9 us
    dot_general x1, matrix products, on_device(): jnp.einsum('fyx,xk->fyk', tendency, forward_x, preferred_element_type=jnp...  13.9 us
    dot_general x1, matrix products, on_device(): jnp.einsum('fyk,kx->fyx', gathered, inverse_x, preferred_element_type=jnp...  12.3 us
    dot_general x1, matrix products, on_device(): jnp.einsum('ky,fyc->fkc', forward_y, returned, preferred_element_type=jnp...  12.3 us
    dot_general x1, matrix products, on_device(): jnp.einsum('yk,fkc->fyc', inverse_y, spectra, preferred_element_type=jnp....  10 us
    all_to_all x1, starting transfers between devices, moved_by_axis(): lax.all_to_all(tiles, axes[k], split_axis=k, concat_axis=k, tiled=True)  7.45 us
  transfers between devices with their start and end apart: 2, of which 2 were waited for; matrix products, arithmetic and copies ran while one was open for 1% of the time, Pallas kernels for 0%

commit v1 on v0

v1 whole, which is shorter than its diff:
```python
import functools
import math

import jax
import jax.numpy as jnp
import ml_dtypes
import numpy as np
from jax import lax
from jax.experimental import pallas as pl
from jax.experimental.pallas import tpu as pltpu
from jax.sharding import PartitionSpec as P

MESH = pl.DeviceIdType.MESH
N = 3072
M = 1024
MODES = 2 * M
NQ = 3
LINES = N // (16 * NQ)
ROWS = 16 * LINES
TILE = 256


def fourier_table():
    point = np.arange(N, dtype=np.int64)
    wave = np.arange(1, M + 1, dtype=np.int64)
    angle = (point[:, None] * wave[None, :] % N).astype(np.float64) * (2.0 * math.pi / N)
    table = np.concatenate([np.cos(angle), np.sin(angle)], 1) / math.sqrt(M)
    return table.astype(ml_dtypes.bfloat16)


def device_at(y, z, x, core):
    return (y * 2 + z % 2, z // 2 * 8 + x * 2 + core)


def round_trip(
    coupling, spectra, by_point, by_mode, out,
    spec, points, modes, sent1, got1, lines, tend, sent2, got2, total,
    load_sem, send_sem, recv_sem,
):
    row, col = lax.axis_index("row"), lax.axis_index("col")
    y, parity = row // 2, row % 2
    z_hi, x, core = col // 8, col // 2 % 4, col % 2
    other = 1 - parity
    mine = x * 4 + z_hi * 2 + core

    def partner(xp, zp, cp):
        return device_at(y, zp * 2 + other, xp, cp)

    loads = [
        pltpu.make_async_copy(spectra.at[f], spec.at[:, pl.ds(f * 128, 128)], load_sem.at[f])
        for f in range(2)
    ]
    loads += [
        pltpu.make_async_copy(
            by_point.at[pl.ds(q * ROWS, ROWS)], points.at[pl.ds(q * ROWS, ROWS)], load_sem.at[2 + q]
        )
        for q in range(NQ)
    ]
    loads.append(pltpu.make_async_copy(by_mode, modes, load_sem.at[2 + NQ]))
    for load in loads:
        load.start()

    barrier = pltpu.get_barrier_semaphore()
    for xp in range(4):
        for zp in range(2):
            for cp in range(2):
                pl.semaphore_signal(
                    barrier, inc=1, device_id=partner(xp, zp, cp), device_id_type=MESH
                )
    pl.semaphore_wait(barrier, 16)
    loads[0].wait()
    loads[1].wait()

    def whole(leg, q):
        sent, got = ((sent1, got1), (sent2, got2))[leg]
        return pltpu.make_async_remote_copy(
            sent.at[q], got.at[q], send_sem.at[leg, q], recv_sem.at[leg, q],
            device_id=partner(x, 0, core), device_id_type=MESH,
        )

    for q in range(NQ):
        loads[2 + q].wait()

        @pl.loop(0, 4)
        def _(i):
            xo = (x + 2 + 3 * i) % 4
            start = pl.multiple_of(q * ROWS + xo * 4 * LINES, 4 * LINES)
            half = jnp.dot(
                points[pl.ds(start, 4 * LINES), :], spec[...], preferred_element_type=jnp.float32
            ).astype(jnp.bfloat16)
            sent1[q, pl.ds(xo * 4, 4)] = half.reshape(4, LINES, 256)
            for zo in range(2):
                for co in range(2):
                    pltpu.make_async_remote_copy(
                        sent1.at[q, xo * 4 + zo * 2 + co], got1.at[q, col],
                        send_sem.at[0, q], recv_sem.at[0, q],
                        device_id=partner(xo, zo, co), device_id_type=MESH,
                    ).start()

    loads[2 + NQ].wait()
    field = (y * 2 + other) * 2
    strengths = (coupling[field], coupling[field + 1])

    for q in range(NQ):
        whole(0, q).wait_recv()
        for f in range(2):
            for s in range(16):
                lines[f * LINES : (f + 1) * LINES, s * 128 : (s + 1) * 128] = got1[
                    q, s, :, f * 128 : (f + 1) * 128
                ]

        @pl.loop(0, N // TILE)
        def _(n):
            cols = pl.ds(pl.multiple_of(n * TILE, TILE), TILE)
            grid = jnp.dot(lines[...], modes[:, cols], preferred_element_type=jnp.float32)
            for f in range(2):
                g = grid[f * LINES : (f + 1) * LINES]
                tend[f * LINES : (f + 1) * LINES, cols] = (g + strengths[f] * g * g).astype(
                    jnp.bfloat16
                )

        @pl.loop(0, 8)
        def _(i):
            zd, xd = i % 2, (x + 2 + 3 * (i // 2)) % 4
            n = zd * 4 + xd
            cols = pl.ds(pl.multiple_of(n * TILE, TILE), TILE)
            back = jnp.dot(tend[...], points[:, cols], preferred_element_type=jnp.float32)
            back = (back * (2.0 / 3.0)).astype(jnp.bfloat16)
            for cd in range(2):
                for f in range(2):
                    sent2[q, 2 * n + cd, :, f * 128 : (f + 1) * 128] = back[
                        f * LINES : (f + 1) * LINES, cd * 128 : (cd + 1) * 128
                    ]
                pltpu.make_async_remote_copy(
                    sent2.at[q, 2 * n + cd], got2.at[q, mine],
                    send_sem.at[1, q], recv_sem.at[1, q],
                    device_id=partner(xd, zd, cd), device_id_type=MESH,
                ).start()

    for q in range(NQ):
        whole(1, q).wait_recv()

        @pl.loop(0, MODES // TILE)
        def _(m):
            rows = pl.ds(pl.multiple_of(m * TILE, TILE), TILE)
            part = jnp.dot(
                modes[rows, q * ROWS : (q + 1) * ROWS],
                got2[q].reshape(ROWS, 256),
                preferred_element_type=jnp.float32,
            )
            if q > 0:
                part = part + total[rows, :]
            if q < NQ - 1:
                total[rows, :] = part
            else:
                part = (part * (2.0 / 3.0)).astype(jnp.bfloat16)
                for f in range(2):
                    out[f, rows, :] = part[:, f * 128 : (f + 1) * 128]

    for q in range(NQ):
        whole(0, q).wait_send()
        whole(1, q).wait_send()


def on_device(spectra, coupling):
    table = fourier_table()
    width = spectra.shape[2]
    anywhere = pl.BlockSpec(memory_space=pl.ANY)
    result = pl.pallas_call(
        round_trip,
        out_shape=jax.ShapeDtypeStruct(spectra.shape, jnp.bfloat16),
        in_specs=[pl.BlockSpec(memory_space=pltpu.SMEM), anywhere, anywhere, anywhere],
        out_specs=pl.BlockSpec(memory_space=pltpu.VMEM),
        scratch_shapes=[
            pltpu.VMEM((MODES, 256), jnp.bfloat16),
            pltpu.VMEM((N, MODES), jnp.bfloat16),
            pltpu.VMEM((MODES, N), jnp.bfloat16),
            pltpu.VMEM((NQ, 16, LINES, 256), jnp.bfloat16),
            pltpu.VMEM((NQ, 16, LINES, 256), jnp.bfloat16),
            pltpu.VMEM((2 * LINES, MODES), jnp.bfloat16),
            pltpu.VMEM((2 * LINES, N), jnp.bfloat16),
            pltpu.VMEM((NQ, 16, LINES, 256), jnp.bfloat16),
            pltpu.VMEM((NQ, 16, LINES, 256), jnp.bfloat16),
            pltpu.VMEM((MODES, 256), jnp.float32),
            pltpu.SemaphoreType.DMA((3 + NQ,)),
            pltpu.SemaphoreType.DMA((2, NQ)),
            pltpu.SemaphoreType.DMA((2, NQ)),
        ],
        compiler_params=pltpu.CompilerParams(
            collective_id=0, has_side_effects=True, vmem_limit_bytes=58 * 1024 * 1024
        ),
        cost_estimate=pl.CostEstimate(
            flops=16_000_000_000, bytes_accessed=30_000_000, transcendentals=0
        ),
    )(coupling, spectra, table, np.ascontiguousarray(table.T))
    kx = (lax.axis_index("col") * width + jnp.arange(width, dtype=jnp.int32)) % M + 1
    ky = jnp.arange(MODES, dtype=jnp.int32) % M + 1
    inside = ky[:, None] * ky[:, None] + kx[None, :] * kx[None, :] <= M * M
    return jnp.where(inside[None], result, jnp.zeros_like(result))


def solution(mesh):
    return jax.shard_map(
        on_device,
        mesh=mesh,
        in_specs=(P("row", None, "col"), P()),
        out_specs=P("row", None, "col"),
        check_vma=False,
    )
```

time: 183 us -> 54.3 us (0.30)
  Pallas kernels: 0 us -> 51.5 us
  other arithmetic: 53.8 us -> 2.69 us
  waiting for transfers between devices: 50.2 us -> 0 us
  matrix products: 48.6 us -> 0 us
  starting transfers between devices: 12.1 us -> 0 us
  local copies, waits for them, and re-layouts: 11.6 us -> 0 us
  blocking collectives: 6 us -> 0 us
    cos x1 -> x0, other arithmetic: 52.6 us -> none  [fourier_rows(): table = jnp.concatenate([jnp.cos(angles), jnp.sin(angles)], 0) * factor]
    pallas_call x0 -> x1, Pallas kernels: none -> 51.5 us  [on_device(): pl.pallas_call(round_trip, out_shape=jax.ShapeDtypeStruct(spectra.shape,...]
    all_to_all x2 -> x0, waiting for transfers between devices: 50.2 us -> none  [the longest x1 27.3 us: on_device(): lax.all_to_all(projected, COL, split_axis=2, concat_axis=1, tiled=True)]
    dot_general x4 -> x0, matrix products: 48.6 us -> none  [the longest x1 13.9 us: on_device(): jnp.einsum('fyx,xk->fyk', tendency, forward_x, preferred_element_type=jnp...]
    all_to_all x2 -> x0, starting transfers between devices: 12.1 us -> none  [the longest x1 7.45 us: moved_by_axis(): lax.all_to_all(tiles, axes[k], split_axis=k, concat_axis=k, tiled=True)]
    all_to_all x3 -> x0, local copies, waits for them, and re-layouts: 6.26 us -> none  [the longest x1 3.66 us: on_device(): lax.all_to_all(projected, COL, split_axis=2, concat_axis=1, tiled=True)]
    all_to_all x1 -> x0, blocking collectives: 6 us -> none  [moved_by_axis(): lax.all_to_all(tiles, axes[k], split_axis=k, concat_axis=k, tiled=True)]
    convert_element_type x2 -> x0, local copies, waits for them, and re-layouts: 5.14 us -> none  [the longest x1 3.83 us: on_device(): projected = jnp.einsum('fyx,xk->fyk', tendency, forward_x, preferred_elem...]
  transfers between devices with their start and end apart: 2 -> 0, of which waited for: 2 -> 0; matrix products, arithmetic and copies ran while one was open for 1% -> 0% of each run, Pallas kernels for 0% -> 0%
where the time goes in v1:
time: 54.3 us; the launch traced here: 54.2 us
  Pallas kernels  51.5 us (95%)
  other arithmetic  2.69 us (5%)
    pallas_call x1, Pallas kernels, on_device(): pl.pallas_call(round_trip, out_shape=jax.ShapeDtypeStruct(spectra.shape,...  51.5 us
    select_n x1, other arithmetic, on_device(): return jnp.where(inside[None], result, jnp.zeros_like(result))  2.33 us

profile of v1, /device:TPU:1, one launch (start us, length us, event | category | flops | bytes accessed | tf_op | source)
XLA Modules:
  0.0 54.2 jit_solution(8908155357750335178)
XLA Ops:
  0.0 0.3 add_compare_fusion
  0.4 51.5 %shard_map.46 = bf16[2,2048,128]{2,1,0:T(8,128)(2,1)} custom-call(f32[16]{0:T(128)} %coupling.1, bf16[2,2048,128]{2,1,0:T(8,128)(2,1)} %spectra.1, bf16[3072,2048]{1,0:T(8,128)(2,1)} %constant.41.clone.by_point, bf16[2048,3072]{1,0:T(8,128)(2,1)} %constant.42.clone.by_mode), custom_call_target="tpu_custom_call" | custom-call | flops 16000000000 | bytes 30000000 | tf_op jit(solution)/shard_map/pallas_call | solution.py:169
  51.9 2.3 %broadcast_select_fusion = bf16[2,2048,128]{2,1,0:T(8,128)(2,1)} fusion(bf16[2,2048,128]{2,1,0:T(8,128)(2,1)} %shard_map.46, pred[2048,128]{1,0:T(8,128)(4,1)S(1)} %add_compare_fusion), kind=kLoop, calls=%fused_computation.1 | loop fusion | flops 524288 | bytes 2359296 | tf_op jit(solution)/shard_map/jit(_where)/select_n | solution.py:199
  (2 shorter events, 0.0 us)

commit v2 on v1

--- a/solution.py
+++ b/solution.py
@@ -33,9 +33,9 @@
 
 
 def round_trip(
-    coupling, spectra, by_point, by_mode, out,
-    spec, points, modes, sent1, got1, lines, tend, sent2, got2, total,
-    load_sem, send_sem, recv_sem,
+    coupling_hbm, spectra, by_point, by_mode, out,
+    coupling, spec, points, modes, sent1, got1, lines, tend, sent2, got2, total,
+    load_sem, send_sem, recv_sem, last_sem,
 ):
     row, col = lax.axis_index("row"), lax.axis_index("col")
     y, parity = row // 2, row % 2
@@ -50,13 +50,19 @@
         pltpu.make_async_copy(spectra.at[f], spec.at[:, pl.ds(f * 128, 128)], load_sem.at[f])
         for f in range(2)
     ]
+    for i in range(4):
+        first = pl.ds(pl.multiple_of((x + 2 + 3 * i) % 4 * 4 * LINES, 4 * LINES), 4 * LINES)
+        loads.append(
+            pltpu.make_async_copy(by_point.at[first], points.at[first], load_sem.at[2 + i])
+        )
     loads += [
         pltpu.make_async_copy(
-            by_point.at[pl.ds(q * ROWS, ROWS)], points.at[pl.ds(q * ROWS, ROWS)], load_sem.at[2 + q]
-        )
-        for q in range(NQ)
+            by_point.at[pl.ds(q * ROWS, ROWS)], points.at[pl.ds(q * ROWS, ROWS)], load_sem.at[5 + q]
+        )
+        for q in range(1, NQ)
     ]
-    loads.append(pltpu.make_async_copy(by_mode, modes, load_sem.at[2 + NQ]))
+    loads.append(pltpu.make_async_copy(by_mode, modes, load_sem.at[5 + NQ]))
+    loads.append(pltpu.make_async_copy(coupling_hbm, coupling, load_sem.at[6 + NQ]))
     for load in loads:
         load.start()
 
@@ -78,26 +84,48 @@
             device_id=partner(x, 0, core), device_id_type=MESH,
         )
 
+    def last_part(xs):
+        return pltpu.make_async_remote_copy(
+            sent2.at[NQ - 1, pl.ds(0, 4)], got2.at[NQ - 1, pl.ds(xs * 4, 4)],
+            send_sem.at[1, NQ - 1], last_sem.at[xs],
+            device_id=partner(x, 0, core), device_id_type=MESH,
+        )
+
+    def to_rows(q, i):
+        xo = (x + 2 + 3 * i) % 4
+        start = pl.multiple_of(q * ROWS + xo * 4 * LINES, 4 * LINES)
+        half = jnp.dot(
+            points[pl.ds(start, 4 * LINES), :], spec[...], preferred_element_type=jnp.float32
+        ).astype(jnp.bfloat16)
+        sent1[q, pl.ds(xo * 4, 4)] = half.reshape(4, LINES, 256)
+
+    def send_rows(q, i):
+        xo = (x + 2 + 3 * i) % 4
+        for zo in range(2):
+            for co in range(2):
+                pltpu.make_async_remote_copy(
+                    sent1.at[q, xo * 4 + zo * 2 + co], got1.at[q, col],
+                    send_sem.at[0, q], recv_sem.at[0, q],
+                    device_id=partner(xo, zo, co), device_id_type=MESH,
+                ).start()
+
     for q in range(NQ):
-        loads[2 + q].wait()
-
-        @pl.loop(0, 4)
-        def _(i):
-            xo = (x + 2 + 3 * i) % 4
-            start = pl.multiple_of(q * ROWS + xo * 4 * LINES, 4 * LINES)
-            half = jnp.dot(
-                points[pl.ds(start, 4 * LINES), :], spec[...], preferred_element_type=jnp.float32
-            ).astype(jnp.bfloat16)
-            sent1[q, pl.ds(xo * 4, 4)] = half.reshape(4, LINES, 256)
-            for zo in range(2):
-                for co in range(2):
-                    pltpu.make_async_remote_copy(
-                        sent1.at[q, xo * 4 + zo * 2 + co], got1.at[q, col],
-                        send_sem.at[0, q], recv_sem.at[0, q],
-                        device_id=partner(xo, zo, co), device_id_type=MESH,
-                    ).start()
-
-    loads[2 + NQ].wait()
+        if q == 0:
+            for i in range(4):
+                loads[2 + i].wait()
+                to_rows(q, i)
+                send_rows(q, i)
+        else:
+            loads[5 + q].wait()
+            for i in range(4):
+                to_rows(q, i)
+
+            @pl.loop(0, 4)
+            def _(i):
+                send_rows(q, i)
+
+    loads[5 + NQ].wait()
+    loads[6 + NQ].wait()
     field = (y * 2 + other) * 2
     strengths = (coupling[field], coupling[field + 1])
 
@@ -109,7 +137,7 @@
                     q, s, :, f * 128 : (f + 1) * 128
                 ]
 
-        @pl.loop(0, N // TILE)
+        @pl.loop(0, N // TILE, unroll=4)
         def _(n):
             cols = pl.ds(pl.multiple_of(n * TILE, TILE), TILE)
             grid = jnp.dot(lines[...], modes[:, cols], preferred_element_type=jnp.float32)
@@ -119,8 +147,7 @@
                     jnp.bfloat16
                 )
 
-        @pl.loop(0, 8)
-        def _(i):
+        def to_modes(i):
             zd, xd = i % 2, (x + 2 + 3 * (i // 2)) % 4
             n = zd * 4 + xd
             cols = pl.ds(pl.multiple_of(n * TILE, TILE), TILE)
@@ -131,16 +158,38 @@
                     sent2[q, 2 * n + cd, :, f * 128 : (f + 1) * 128] = back[
                         f * LINES : (f + 1) * LINES, cd * 128 : (cd + 1) * 128
                     ]
+
+        def send_modes(i):
+            zd, xd = i % 2, (x + 2 + 3 * (i // 2)) % 4
+            n = zd * 4 + xd
+            for cd in range(2):
                 pltpu.make_async_remote_copy(
                     sent2.at[q, 2 * n + cd], got2.at[q, mine],
-                    send_sem.at[1, q], recv_sem.at[1, q],
+                    send_sem.at[1, q], last_sem.at[x] if q == NQ - 1 else recv_sem.at[1, q],
                     device_id=partner(xd, zd, cd), device_id_type=MESH,
                 ).start()
 
-    for q in range(NQ):
+        @pl.loop(0, 2)
+        def _(h):
+            for i in range(4):
+                to_modes(h * 4 + i)
+            for i in range(4):
+                send_modes(h * 4 + i)
+
+    kx = (col * 128 + lax.broadcasted_iota(jnp.int32, (1, 128), 1)) % M + 1
+
+    def finish(rows, start, part):
+        part = (part * (2.0 / 3.0)).astype(jnp.bfloat16)
+        ky = (start + lax.broadcasted_iota(jnp.int32, (TILE, 1), 0)) % M + 1
+        inside = kx * kx + ky * ky <= M * M
+        for f in range(2):
+            kept = jnp.where(inside, part[:, f * 128 : (f + 1) * 128], 0.0)
+            out[f, rows, :] = kept.astype(jnp.bfloat16)
+
+    for q in range(NQ - 1):
         whole(1, q).wait_recv()
 
-        @pl.loop(0, MODES // TILE)
+        @pl.loop(0, MODES // TILE, unroll=4)
         def _(m):
             rows = pl.ds(pl.multiple_of(m * TILE, TILE), TILE)
             part = jnp.dot(
@@ -150,12 +199,26 @@
             )
             if q > 0:
                 part = part + total[rows, :]
-            if q < NQ - 1:
+            total[rows, :] = part
+
+    for j in range(4):
+        xs = (x + 2 + j) % 4
+        last_part(xs).wait_recv()
+        cols = pl.ds(pl.multiple_of((NQ - 1) * ROWS + xs * 4 * LINES, 4 * LINES), 4 * LINES)
+
+        @pl.loop(0, MODES // TILE, unroll=4)
+        def _(m):
+            start = pl.multiple_of(m * TILE, TILE)
+            rows = pl.ds(start, TILE)
+            part = total[rows, :] + jnp.dot(
+                modes[rows, cols],
+                got2[NQ - 1, pl.ds(xs * 4, 4)].reshape(4 * LINES, 256),
+                preferred_element_type=jnp.float32,
+            )
+            if j < 3:
                 total[rows, :] = part
             else:
-                part = (part * (2.0 / 3.0)).astype(jnp.bfloat16)
-                for f in range(2):
-                    out[f, rows, :] = part[:, f * 128 : (f + 1) * 128]
+                finish(rows, start, part)
 
     for q in range(NQ):
         whole(0, q).wait_send()
@@ -164,14 +227,14 @@
 
 def on_device(spectra, coupling):
     table = fourier_table()
-    width = spectra.shape[2]
-    anywhere = pl.BlockSpec(memory_space=pl.ANY)
-    result = pl.pallas_call(
+    in_hbm = pl.BlockSpec(memory_space=pltpu.HBM)
+    return pl.pallas_call(
         round_trip,
         out_shape=jax.ShapeDtypeStruct(spectra.shape, jnp.bfloat16),
-        in_specs=[pl.BlockSpec(memory_space=pltpu.SMEM), anywhere, anywhere, anywhere],
+        in_specs=[in_hbm] * 4,
         out_specs=pl.BlockSpec(memory_space=pltpu.VMEM),
         scratch_shapes=[
+            pltpu.SMEM((16,), jnp.float32),
             pltpu.VMEM((MODES, 256), jnp.bfloat16),
             pltpu.VMEM((N, MODES), jnp.bfloat16),
             pltpu.VMEM((MODES, N), jnp.bfloat16),
@@ -182,21 +245,18 @@
             pltpu.VMEM((NQ, 16, LINES, 256), jnp.bfloat16),
             pltpu.VMEM((NQ, 16, LINES, 256), jnp.bfloat16),
             pltpu.VMEM((MODES, 256), jnp.float32),
-            pltpu.SemaphoreType.DMA((3 + NQ,)),
+            pltpu.SemaphoreType.DMA((7 + NQ,)),
             pltpu.SemaphoreType.DMA((2, NQ)),
             pltpu.SemaphoreType.DMA((2, NQ)),
+            pltpu.SemaphoreType.DMA((4,)),
         ],
         compiler_params=pltpu.CompilerParams(
-            collective_id=0, has_side_effects=True, vmem_limit_bytes=58 * 1024 * 1024
+            collective_id=0, has_side_effects=True, vmem_limit_bytes=48 * 1024 * 1024
         ),
         cost_estimate=pl.CostEstimate(
             flops=16_000_000_000, bytes_accessed=30_000_000, transcendentals=0
         ),
-    )(coupling, spectra, table, np.ascontiguousarray(table.T))
-    kx = (lax.axis_index("col") * width + jnp.arange(width, dtype=jnp.int32)) % M + 1
-    ky = jnp.arange(MODES, dtype=jnp.int32) % M + 1
-    inside = ky[:, None] * ky[:, None] + kx[None, :] * kx[None, :] <= M * M
-    return jnp.where(inside[None], result, jnp.zeros_like(result))
+    )(*(pltpu.with_memory_space_constraint(a, pltpu.HBM) for a in (coupling, spectra)), table, np.ascontiguousarray(table.T))
 
 
 def solution(mesh):

time: 54.3 us -> 47 us (0.87)
  Pallas kernels: 51.5 us -> 45.9 us
  other arithmetic: 2.69 us -> 0 us
  local copies, waits for them, and re-layouts: 0 us -> 0.97 us
    pallas_call x1, Pallas kernels: 51.5 us -> 45.9 us  [on_device(): pl.pallas_call(round_trip, out_shape=jax.ShapeDtypeStruct(spectra.shape,...]
    select_n x1 -> x0, other arithmetic: 2.33 us -> none  [on_device(): return jnp.where(inside[None], result, jnp.zeros_like(result))]
    unnamed x0 -> x1, local copies, waits for them, and re-layouts: none -> 0.97 us
where the time goes in v2:
time: 47 us; the launch traced here: 46.9 us
  Pallas kernels  45.9 us (98%)
  local copies, waits for them, and re-layouts  0.97 us (2%)
    pallas_call x1, Pallas kernels, on_device(): pl.pallas_call(round_trip, out_shape=jax.ShapeDtypeStruct(spectra.shape,...  45.9 us
    unnamed x1, local copies, waits for them, and re-layouts  0.97 us

profile of v2, /device:TPU:1, one launch (start us, length us, event | category | flops | bytes accessed | tf_op | source)
XLA Modules:
  0.0 46.9 jit_solution(12716533272338228989)
XLA Ops:
  0.0 45.9 %shard_map.46 = bf16[2,2048,128]{2,1,0:T(8,128)(2,1)S(1)} custom-call(f32[16]{0:T(128)} %coupling_hbm.1, bf16[2,2048,128]{2,1,0:T(8,128)(2,1)} %spectra.1, bf16[3072,2048]{1,0:T(8,128)(2,1)} %constant.4.clone.by_point, bf16[2048,3072]{1,0:T(8,128)(2,1)} %constant.5.clone.by_mode), custom_call_target="tpu_custom_call" | custom-call | flops 16000000000 | bytes 30000000 | tf_op jit(solution)/shard_map/pallas_call | solution.py:231
  46.0 1.0 %copy.6 = bf16[2,2048,128]{2,1,0:T(8,128)(2,1)} copy(bf16[2,2048,128]{2,1,0:T(8,128)(2,1)S(1)} %shard_map.46) | data formatting | bytes 2097152

commit v3 on v2

--- a/solution.py
+++ b/solution.py
@@ -14,6 +14,7 @@
 N = 3072
 M = 1024
 MODES = 2 * M
+EARLY = 1
 NQ = 3
 LINES = N // (16 * NQ)
 ROWS = 16 * LINES
@@ -42,6 +43,13 @@
     z_hi, x, core = col // 8, col // 2 % 4, col % 2
     other = 1 - parity
     mine = x * 4 + z_hi * 2 + core
+    z = z_hi * 2 + parity
+
+    def x_at(i):
+        return (x + (1, 3, 2, 0)[i]) % 4
+
+    def z_at(up):
+        return (z + 1 + 2 * (up % 2)) % 4 // 2
 
     def partner(xp, zp, cp):
         return device_at(y, zp * 2 + other, xp, cp)
@@ -51,7 +59,7 @@
         for f in range(2)
     ]
     for i in range(4):
-        first = pl.ds(pl.multiple_of((x + 2 + 3 * i) % 4 * 4 * LINES, 4 * LINES), 4 * LINES)
+        first = pl.ds(pl.multiple_of(x_at(i) * 4 * LINES, 4 * LINES), 4 * LINES)
         loads.append(
             pltpu.make_async_copy(by_point.at[first], points.at[first], load_sem.at[2 + i])
         )
@@ -73,7 +81,6 @@
                 pl.semaphore_signal(
                     barrier, inc=1, device_id=partner(xp, zp, cp), device_id_type=MESH
                 )
-    pl.semaphore_wait(barrier, 16)
     loads[0].wait()
     loads[1].wait()
 
@@ -92,37 +99,41 @@
         )
 
     def to_rows(q, i):
-        xo = (x + 2 + 3 * i) % 4
+        xo = x_at(i)
         start = pl.multiple_of(q * ROWS + xo * 4 * LINES, 4 * LINES)
         half = jnp.dot(
             points[pl.ds(start, 4 * LINES), :], spec[...], preferred_element_type=jnp.float32
         ).astype(jnp.bfloat16)
         sent1[q, pl.ds(xo * 4, 4)] = half.reshape(4, LINES, 256)
 
-    def send_rows(q, i):
-        xo = (x + 2 + 3 * i) % 4
-        for zo in range(2):
-            for co in range(2):
-                pltpu.make_async_remote_copy(
-                    sent1.at[q, xo * 4 + zo * 2 + co], got1.at[q, col],
-                    send_sem.at[0, q], recv_sem.at[0, q],
-                    device_id=partner(xo, zo, co), device_id_type=MESH,
-                ).start()
-
-    for q in range(NQ):
-        if q == 0:
+    def send_rows(q, i, up):
+        xo, zo = x_at(i), z_at(up)
+        for co in range(2):
+            pltpu.make_async_remote_copy(
+                sent1.at[q, xo * 4 + zo * 2 + co], got1.at[q, col],
+                send_sem.at[0, q], recv_sem.at[0, q],
+                device_id=partner(xo, zo, co), device_id_type=MESH,
+            ).start()
+
+    for i in range(EARLY):
+        loads[2 + i].wait()
+        to_rows(0, i)
+    pl.semaphore_wait(barrier, 16)
+    for up in range(2):
+        for i in range(EARLY):
+            send_rows(0, i, i + up)
+    for i in range(EARLY, 4):
+        loads[2 + i].wait()
+        to_rows(0, i)
+        send_rows(0, i, i)
+        send_rows(0, i, i + 1)
+    for q in range(1, NQ):
+        loads[5 + q].wait()
+        for i in range(4):
+            to_rows(q, i)
+        for up in range(2):
             for i in range(4):
-                loads[2 + i].wait()
-                to_rows(q, i)
-                send_rows(q, i)
-        else:
-            loads[5 + q].wait()
-            for i in range(4):
-                to_rows(q, i)
-
-            @pl.loop(0, 4)
-            def _(i):
-                send_rows(q, i)
+                send_rows(q, i, i + up)
 
     loads[5 + NQ].wait()
     loads[6 + NQ].wait()
@@ -147,8 +158,8 @@
                     jnp.bfloat16
                 )
 
-        def to_modes(i):
-            zd, xd = i % 2, (x + 2 + 3 * (i // 2)) % 4
+        def to_modes(h, i):
+            zd, xd = z_at(h + i), x_at(i)
             n = zd * 4 + xd
             cols = pl.ds(pl.multiple_of(n * TILE, TILE), TILE)
             back = jnp.dot(tend[...], points[:, cols], preferred_element_type=jnp.float32)
@@ -159,8 +170,8 @@
                         f * LINES : (f + 1) * LINES, cd * 128 : (cd + 1) * 128
                     ]
 
-        def send_modes(i):
-            zd, xd = i % 2, (x + 2 + 3 * (i // 2)) % 4
+        def send_modes(h, i):
+            zd, xd = z_at(h + i), x_at(i)
             n = zd * 4 + xd
             for cd in range(2):
                 pltpu.make_async_remote_copy(
@@ -172,9 +183,9 @@
         @pl.loop(0, 2)
         def _(h):
             for i in range(4):
-                to_modes(h * 4 + i)
+                to_modes(h, i)
             for i in range(4):
-                send_modes(h * 4 + i)
+                send_modes(h, i)
 
     kx = (col * 128 + lax.broadcasted_iota(jnp.int32, (1, 128), 1)) % M + 1
 
@@ -202,7 +213,7 @@
             total[rows, :] = part
 
     for j in range(4):
-        xs = (x + 2 + j) % 4
+        xs = (x + (3, 1, 2, 0)[j]) % 4
         last_part(xs).wait_recv()
         cols = pl.ds(pl.multiple_of((NQ - 1) * ROWS + xs * 4 * LINES, 4 * LINES), 4 * LINES)
 

time: 47 us -> 46.3 us (0.985)
  Pallas kernels: 45.9 us -> 45.2 us
    pallas_call x1, Pallas kernels: 45.9 us -> 45.2 us  [on_device(): pl.pallas_call(round_trip, out_shape=jax.ShapeDtypeStruct(spectra.shape,...]
where the time goes in v3:
time: 46.3 us; the launch traced here: 46.2 us
  Pallas kernels  45.2 us (98%)
  local copies, waits for them, and re-layouts  0.97 us (2%)
    pallas_call x1, Pallas kernels, on_device(): pl.pallas_call(round_trip, out_shape=jax.ShapeDtypeStruct(spectra.shape,...  45.2 us
    unnamed x1, local copies, waits for them, and re-layouts  0.97 us

profile of v3, /device:TPU:1, one launch (start us, length us, event | category | flops | bytes accessed | tf_op | source)
XLA Modules:
  0.0 46.2 jit_solution(2580452935894581435)
XLA Ops:
  0.0 45.2 %shard_map.46 = bf16[2,2048,128]{2,1,0:T(8,128)(2,1)S(1)} custom-call(f32[16]{0:T(128)} %coupling_hbm.1, bf16[2,2048,128]{2,1,0:T(8,128)(2,1)} %spectra.1, bf16[3072,2048]{1,0:T(8,128)(2,1)} %constant.4.clone.by_point, bf16[2048,3072]{1,0:T(8,128)(2,1)} %constant.5.clone.by_mode), custom_call_target="tpu_custom_call" | custom-call | flops 16000000000 | bytes 30000000 | tf_op jit(solution)/shard_map/pallas_call | solution.py:242
  45.2 1.0 %copy.6 = bf16[2,2048,128]{2,1,0:T(8,128)(2,1)} copy(bf16[2,2048,128]{2,1,0:T(8,128)(2,1)S(1)} %shard_map.46) | data formatting | bytes 2097152

commit v4 on v3

--- a/solution.py
+++ b/solution.py
@@ -173,7 +173,7 @@
         def send_modes(h, i):
             zd, xd = z_at(h + i), x_at(i)
             n = zd * 4 + xd
-            for cd in range(2):
+            for cd in (1, 0):
                 pltpu.make_async_remote_copy(
                     sent2.at[q, 2 * n + cd], got2.at[q, mine],
                     send_sem.at[1, q], last_sem.at[x] if q == NQ - 1 else recv_sem.at[1, q],
@@ -182,10 +182,11 @@
 
         @pl.loop(0, 2)
         def _(h):
-            for i in range(4):
-                to_modes(h, i)
-            for i in range(4):
-                send_modes(h, i)
+            for pair in (0, 2):
+                for i in range(2):
+                    to_modes(h, pair + i)
+                for i in range(2):
+                    send_modes(h, pair + i)
 
     kx = (col * 128 + lax.broadcasted_iota(jnp.int32, (1, 128), 1)) % M + 1
 
@@ -217,7 +218,7 @@
         last_part(xs).wait_recv()
         cols = pl.ds(pl.multiple_of((NQ - 1) * ROWS + xs * 4 * LINES, 4 * LINES), 4 * LINES)
 
-        @pl.loop(0, MODES // TILE, unroll=4)
+        @pl.loop(0, MODES // TILE, unroll=8)
         def _(m):
             start = pl.multiple_of(m * TILE, TILE)
             rows = pl.ds(start, TILE)

time: 46.3 us -> 45.3 us (0.978)
  Pallas kernels: 45.2 us -> 44.2 us
    pallas_call x1, Pallas kernels: 45.2 us -> 44.2 us  [on_device(): pl.pallas_call(round_trip, out_shape=jax.ShapeDtypeStruct(spectra.shape,...]
where the time goes in v4:
time: 45.3 us; the launch traced here: 45.2 us
  Pallas kernels  44.2 us (98%)
  local copies, waits for them, and re-layouts  0.97 us (2%)
    pallas_call x1, Pallas kernels, on_device(): pl.pallas_call(round_trip, out_shape=jax.ShapeDtypeStruct(spectra.shape,...  44.2 us
    unnamed x1, local copies, waits for them, and re-layouts  0.97 us

profile of v4, /device:TPU:1, one launch (start us, length us, event | category | flops | bytes accessed | tf_op | source)
XLA Modules:
  0.0 45.2 jit_solution(16413346350806277431)
XLA Ops:
  0.0 44.2 %shard_map.46 = bf16[2,2048,128]{2,1,0:T(8,128)(2,1)S(1)} custom-call(f32[16]{0:T(128)} %coupling_hbm.1, bf16[2,2048,128]{2,1,0:T(8,128)(2,1)} %spectra.1, bf16[3072,2048]{1,0:T(8,128)(2,1)} %constant.4.clone.by_point, bf16[2048,3072]{1,0:T(8,128)(2,1)} %constant.5.clone.by_mode), custom_call_target="tpu_custom_call" | custom-call | flops 16000000000 | bytes 30000000 | tf_op jit(solution)/shard_map/pallas_call | solution.py:243
  44.2 1.0 %copy.6 = bf16[2,2048,128]{2,1,0:T(8,128)(2,1)} copy(bf16[2,2048,128]{2,1,0:T(8,128)(2,1)S(1)} %shard_map.46) | data formatting | bytes 2097152

commit v5 on v4

--- a/solution.py
+++ b/solution.py
@@ -15,6 +15,7 @@
 M = 1024
 MODES = 2 * M
 EARLY = 1
+GROUPS = ((0, 1, 2), (3,))
 NQ = 3
 LINES = N // (16 * NQ)
 ROWS = 16 * LINES
@@ -213,21 +214,24 @@
                 part = part + total[rows, :]
             total[rows, :] = part
 
-    for j in range(4):
-        xs = (x + (3, 1, 2, 0)[j]) % 4
-        last_part(xs).wait_recv()
-        cols = pl.ds(pl.multiple_of((NQ - 1) * ROWS + xs * 4 * LINES, 4 * LINES), 4 * LINES)
+    for group in GROUPS:
+        pieces = [(x + (3, 1, 2, 0)[j]) % 4 for j in group]
+        for xs in pieces:
+            last_part(xs).wait_recv()
 
         @pl.loop(0, MODES // TILE, unroll=8)
         def _(m):
             start = pl.multiple_of(m * TILE, TILE)
             rows = pl.ds(start, TILE)
-            part = total[rows, :] + jnp.dot(
-                modes[rows, cols],
-                got2[NQ - 1, pl.ds(xs * 4, 4)].reshape(4 * LINES, 256),
-                preferred_element_type=jnp.float32,
-            )
-            if j < 3:
+            part = total[rows, :]
+            for xs in pieces:
+                first = pl.multiple_of((NQ - 1) * ROWS + xs * 4 * LINES, 4 * LINES)
+                part += jnp.dot(
+                    modes[rows, pl.ds(first, 4 * LINES)],
+                    got2[NQ - 1, pl.ds(xs * 4, 4)].reshape(4 * LINES, 256),
+                    preferred_element_type=jnp.float32,
+                )
+            if group != GROUPS[-1]:
                 total[rows, :] = part
             else:
                 finish(rows, start, part)

time: 45.3 us -> 45.3 us (level)
  no operation moved by 1% of the time
where the time goes in v5:
time: 45.3 us; the launch traced here: 45.2 us
  Pallas kernels  44.3 us (98%)
  local copies, waits for them, and re-layouts  0.97 us (2%)
    pallas_call x1, Pallas kernels, on_device(): pl.pallas_call(round_trip, out_shape=jax.ShapeDtypeStruct(spectra.shape,...  44.3 us
    unnamed x1, local copies, waits for them, and re-layouts  0.97 us

profile of v5, /device:TPU:1, one launch (start us, length us, event | category | flops | bytes accessed | tf_op | source)
XLA Modules:
  0.0 45.2 jit_solution(11586637637894581195)
XLA Ops:
  0.0 44.3 %shard_map.46 = bf16[2,2048,128]{2,1,0:T(8,128)(2,1)S(1)} custom-call(f32[16]{0:T(128)} %coupling_hbm.1, bf16[2,2048,128]{2,1,0:T(8,128)(2,1)} %spectra.1, bf16[3072,2048]{1,0:T(8,128)(2,1)} %constant.4.clone.by_point, bf16[2048,3072]{1,0:T(8,128)(2,1)} %constant.5.clone.by_mode), custom_call_target="tpu_custom_call" | custom-call | flops 16000000000 | bytes 30000000 | tf_op jit(solution)/shard_map/pallas_call | solution.py:247
  44.3 1.0 %copy.6 = bf16[2,2048,128]{2,1,0:T(8,128)(2,1)} copy(bf16[2,2048,128]{2,1,0:T(8,128)(2,1)S(1)} %shard_map.46) | data formatting | bytes 2097152
